TPU v7x, 32 devices: a whole 2x2x4 slice. The times are simulated.
32 devices in a mesh: groups: 2 (over y), block: 4 (over z), seg: 2 (over x), sub: 2 (over core).
Axes of the slice: x: 2, y: 2, z: 4, core: 2. Of those that a mesh axis runs over, the one named last changes fastest.
Arguments:
- old_fields: float32 [2048, 4, 512], P(('groups', 'block', 'seg', 'sub')), parts along dimension 0, may hold values from -6 to 6
- corner_shift: float32 [24, 2048], P(None, ('groups', 'block', 'seg', 'sub')), parts along dimension 1, may hold values from -0.2 to 0.2
- targets: float32 [3, 131072], P(None, ('groups', 'block', 'seg', 'sub')), parts along dimension 1, may hold values from -0.7 to 0.7
- owners: int32 [1024], P(('groups', 'block', 'seg', 'sub')), parts along dimension 0, may hold values from 0 to 1023, as said below
Outputs:
- new_fields: float32 [4, 131072], P(None, ('groups', 'block', 'seg', 'sub')), parts along dimension 1
There are 2 independent parts, one for each index of `groups`. A program takes and returns all parts, laid end to end along the dimension named above; each array names one. Nothing has to cross between parts.
Inputs may be any that keep to these rules, and one draw needn't show every extreme that they name: `owners`: owner e lies on device e // 64. At most 2 of the blocks on the rows of one device are owned by elements of any one device, and in every draw some device owns exactly 2 blocks of every device.
All inputs are finite; a program needn't handle non-finite values.
Results may differ from a plain program's by a relative error of at most 0.00029.
Values sent between devices are 32-bit elements; how exact they have to be, the bound alone decides.
A program may use at most 64 MiB of HBM per device.

v0:
```python
import jax
import jax.numpy as jnp
import numpy as np
from jax import lax
from jax.sharding import PartitionSpec as P

NEWTON = 3
CAP = 2
GLL_POINTS = (
    -1.0,
    -0.8717401485096066,
    -0.5917001814331423,
    -0.2092992179024789,
    0.2092992179024789,
    0.5917001814331423,
    0.8717401485096066,
    1.0,
)
EXACT = lax.Precision.HIGHEST


def lagrange_rows(coords):
    gll_nodes = jnp.array(GLL_POINTS, jnp.float32)
    offsets = coords[None, :] - gll_nodes[:, None]
    spacing = gll_nodes[:, None] - gll_nodes[None, :] + jnp.eye(8, dtype=jnp.float32)
    diag_mask = jnp.eye(8, dtype=bool)
    factors = jnp.where(diag_mask[:, :, None], 1.0, offsets[None, :, :] / spacing[:, :, None])
    return jnp.prod(factors, axis=1)


def corner_signs():
    bit_table = np.array(
        [[corner >> 2 - coord_dim & 1 for corner in range(8)] for coord_dim in range(3)], np.float32
    )
    return jnp.asarray(2.0 * bit_table - 1.0)


def outer_prod(first, second, third):
    return (first[:, None, None, :] * second[None, :, None, :] * third[None, None, :, :]).reshape(
        8, -1
    )


def trilinear(ref_pos):
    shape_list = []
    slope_list = []
    for coord_dim in range(3):
        coordinate = ref_pos[coord_dim]
        shape_list.append(jnp.stack([0.5 - 0.5 * coordinate, 0.5 + 0.5 * coordinate]))
        slope_list.append(
            jnp.stack([jnp.full_like(coordinate, -0.5), jnp.full_like(coordinate, 0.5)])
        )
    values = outer_prod(shape_list[0], shape_list[1], shape_list[2])
    slopes = [
        outer_prod(slope_list[0], shape_list[1], shape_list[2]),
        outer_prod(shape_list[0], slope_list[1], shape_list[2]),
        outer_prod(shape_list[0], shape_list[1], slope_list[2]),
    ]
    return (values, slopes)


def solve_three(matrix, rhs_rows):
    cofactors = []
    for row_id in range(3):
        keep_rows = [remain for remain in range(3) if remain != row_id]
        cof_row = []
        for col_id in range(3):
            keep_cols = [remain for remain in range(3) if remain != col_id]
            sign_factor = 1.0 if (row_id + col_id) % 2 == 0 else -1.0
            cof_row.append(
                sign_factor
                * (
                    matrix[keep_rows[0]][keep_cols[0]] * matrix[keep_rows[1]][keep_cols[1]]
                    - matrix[keep_rows[0]][keep_cols[1]] * matrix[keep_rows[1]][keep_cols[0]]
                )
            )
        cofactors.append(cof_row)
    determinant = (
        matrix[0][0] * cofactors[0][0]
        + matrix[0][1] * cofactors[0][1]
        + matrix[0][2] * cofactors[0][2]
    )
    return [
        (
            cofactors[0][col_id] * rhs_rows[0]
            + cofactors[1][col_id] * rhs_rows[1]
            + cofactors[2][col_id] * rhs_rows[2]
        )
        / determinant
        for col_id in range(3)
    ]


def invert_map(corners, target):
    ref_pos = jnp.zeros_like(target)
    for iteration in range(NEWTON):
        values, slopes = trilinear(ref_pos)
        mapped = jnp.dot(corners, values, precision=EXACT)
        columns = [jnp.dot(corners, slope_row, precision=EXACT) for slope_row in slopes]
        matrix = [[columns[col_id][row_id] for col_id in range(3)] for row_id in range(3)]
        misfit = mapped - target
        update = solve_three(matrix, [misfit[row_id] for row_id in range(3)])
        ref_pos = jnp.clip(ref_pos - jnp.stack(update), -1.2, 1.2)
    return ref_pos


def interpolate(element_field, corners, target):
    ref_pos = invert_map(corners, target)
    along_x = lagrange_rows(ref_pos[0])
    along_y = lagrange_rows(ref_pos[1])
    along_z = lagrange_rows(ref_pos[2])
    weights = (along_y[:, None, :] * along_z[None, :, :]).reshape(64, -1)
    var_count = element_field.shape[0]
    partial_sum = jnp.dot(element_field.reshape(var_count * 8, 64), weights, precision=EXACT)
    return jnp.sum(partial_sum.reshape(var_count, 8, -1) * along_x[None, :, :], axis=1)


def interpolate_blocks(fields, shifts, points):
    cube_signs = corner_signs()

    def per_block(inputs):
        element_field, shift_row, target = inputs
        return interpolate(element_field, cube_signs + shift_row.reshape(3, 8), target)

    return lax.map(per_block, (fields, shifts, points), batch_size=64)


def slot_table(owners, elems_local, capacity):
    owner_dev = owners // elems_local
    local_elem = owners - owner_dev * elems_local
    block_count = owners.shape[0]
    earlier = jnp.tril(jnp.ones((block_count, block_count), jnp.int32), -1)
    matches = (owner_dev[:, None] == owner_dev[None, :]).astype(jnp.int32)
    arrival = jnp.sum(matches * earlier, axis=1)
    return (owner_dev * capacity + arrival, local_elem)


def shards(old_fields, corner_shift, targets, owners):
    outer_count = lax.axis_size("block")
    inner_count = lax.axis_size("seg") * lax.axis_size("sub")
    slot_count = outer_count * inner_count * CAP
    elems_local = old_fields.shape[0]
    var_count = old_fields.shape[1]
    block_count = owners.shape[0]
    slot_index, local_elem = slot_table(owners, elems_local, CAP)
    block_points = targets.reshape(3, block_count, -1).transpose(1, 0, 2)
    point_count = block_points.shape[2]
    outgoing = jnp.zeros((slot_count, 3, point_count), jnp.float32).at[slot_index].set(block_points)
    wanted = jnp.full((slot_count,), -1, jnp.int32).at[slot_index].set(local_elem)
    arrived, asked = (
        lax.all_to_all(
            lax.all_to_all(
                outgoing.reshape(outer_count, inner_count, CAP, 3, point_count),
                "block",
                split_axis=0,
                concat_axis=0,
                tiled=True,
            ),
            ("seg", "sub"),
            split_axis=1,
            concat_axis=1,
            tiled=True,
        ),
        lax.all_to_all(
            lax.all_to_all(
                wanted.reshape(outer_count, inner_count, CAP),
                "block",
                split_axis=0,
                concat_axis=0,
                tiled=True,
            ),
            ("seg", "sub"),
            split_axis=1,
            concat_axis=1,
            tiled=True,
        ),
    )
    asked = asked.reshape(slot_count)
    live_slot = asked >= 0
    element = jnp.where(live_slot, asked, 0)
    fields = old_fields[element]
    shifts = jnp.transpose(corner_shift[:, element])
    computed = interpolate_blocks(fields, shifts, arrived.reshape(slot_count, 3, point_count))
    computed = jnp.where(live_slot[:, None, None], computed, 0.0)
    returned = lax.all_to_all(
        lax.all_to_all(
            computed.reshape(outer_count, inner_count, CAP, var_count, point_count),
            "block",
            split_axis=0,
            concat_axis=0,
            tiled=True,
        ),
        ("seg", "sub"),
        split_axis=1,
        concat_axis=1,
        tiled=True,
    )
    mine = returned.reshape(slot_count, var_count, point_count)[slot_index]
    return mine.transpose(1, 0, 2).reshape(var_count, -1)


def solution(mesh):
    in_specs = (
        P(("groups", "block", "seg", "sub"), None, None),
        P(None, ("groups", "block", "seg", "sub")),
        P(None, ("groups", "block", "seg", "sub")),
        P(("groups", "block", "seg", "sub")),
    )
    out_specs = P(None, ("groups", "block", "seg", "sub"))
    return jax.shard_map(shards, mesh=mesh, in_specs=in_specs, out_specs=out_specs, check_vma=False)
```

profile of v0, /device:TPU:0, one launch (start us, length us, event | category | flops | bytes accessed | tf_op | source)
XLA Modules:
  0.0 64.6 jit_solution(12692678252523733216)
XLA Ops:
  0.0 0.0 copy-start
  0.0 0.7 %multiply_subtract_fusion.2 = (s32[32]{0:T(128)S(1)}, s32[32]{0:T(128)S(1)}, s32[32]{0:T(128)S(1)}) fusion(s32[32]{0:T(128)} %param.11), kind=kLoop, calls=%fused_computation.237 | loop fusion | flops 576 | bytes 512 | tf_op jit(solution)/shard_map/sub | solution.py:130
  0.7 0.2 select_reduce_fusion
  0.9 0.7 %scatter_custom_fusion = s32[32]{0:T(128)S(1)} fusion(s32[32]{0:T(128)S(1)} %compare_select_fusion.2, s32[32]{0:T(128)S(1)} %get-tuple-element.10, s32[]{:T(128)} %constant.26.clone.1), kind=kCustom, calls=%fused_computation.239 | custom fusion | bytes 132 | tf_op jit(solution)/shard_map/scatter | solution.py:149
  1.6 0.1 reshape.2161
  1.7 0.0 copy-start.3
  1.7 0.0 copy-start.7
  1.7 0.0 copy-start.8
  1.7 0.7 %copy.272 = s32[4,4,2]{1,2,0:T(2,128)} copy(s32[4,4,2]{2,1,0:T(4,128)S(1)} %reshape.2161) | data formatting | bytes 256 | tf_op jit(solution)/shard_map/reshape | solution.py:166
  2.4 6.5 %all-to-all-start = ((s32[4,4,2]{1,2,0:T(2,128)}), s32[4,4,2]{1,2,0:T(2,128)S(1)}, u32[]{:S(2)}, u32[]{:S(2)}) async-start(s32[4,4,2]{1,2,0:T(2,128)} %copy.272), calls=%async_computation | async-start | bytes 8192 | tf_op jit(solution)/shard_map/all_to_all | solution.py:165
  8.9 0.1 copy.277
  9.0 0.0 copy-done.7
  9.0 0.1 add_add_fusion
  9.1 1.5 %scatter_fusion = f32[32,3,128]{2,1,0:T(4,128)S(1)} fusion(f32[32,3,128]{2,1,0:T(4,128)S(1)} %broadcast.569, s32[32]{0:T(128)S(1)} %compare_select_fusion.2, f32[32,3,128]{2,1,0:T(4,128)S(1)} %bitcast.790), kind=kCustom, calls=%fused_computation.4 | custom fusion | bytes 147584 | tf_op jit(solution)/shard_map/scatter | solution.py:148
  10.6 3.9 %all-to-all-done = s32[4,4,2]{1,2,0:T(2,128)S(1)} async-done(((s32[4,4,2]{1,2,0:T(2,128)}), s32[4,4,2]{1,2,0:T(2,128)S(1)}, u32[]{:S(2)}, u32[]{:S(2)}) %all-to-all-start) | async-done | bytes 160 | tf_op jit(solution)/shard_map/all_to_all | solution.py:165
  14.5 0.7 %copy.273 = s32[4,4,2]{0,2,1:T(2,128)} copy(s32[4,4,2]{1,2,0:T(2,128)S(1)} %all-to-all-done) | data formatting | bytes 256 | tf_op jit(solution)/shard_map/all_to_all | solution.py:165
  15.2 3.2 %all-to-all-start.1 = ((s32[4,4,2]{0,2,1:T(2,128)}), s32[4,4,2]{0,2,1:T(2,128)S(1)}, u32[]{:S(2)}, u32[]{:S(2)}) async-start(s32[4,4,2]{0,2,1:T(2,128)} %copy.273), calls=%async_computation.1 | async-start | bytes 8192 | tf_op jit(solution)/shard_map/all_to_all | solution.py:164
  18.4 0.6 %copy.281 = f32[4,4,2,3,128]{4,2,1,3,0:T(2,128)} copy(f32[4,4,2,3,128]{4,3,2,1,0:T(4,128)S(1)} %bitcast.767) | data formatting | bytes 98304 | tf_op jit(solution)/shard_map/reshape | solution.py:153
  19.1 3.1 %all-to-all-done.1 = s32[4,4,2]{0,2,1:T(2,128)S(1)} async-done(((s32[4,4,2]{0,2,1:T(2,128)}), s32[4,4,2]{0,2,1:T(2,128)S(1)}, u32[]{:S(2)}, u32[]{:S(2)}) %all-to-all-start.1) | async-done | bytes 160 | tf_op jit(solution)/shard_map/all_to_all | solution.py:164
  22.2 3.3 %all-to-all-start.2 = ((f32[4,4,2,3,128]{4,2,1,3,0:T(2,128)}), f32[4,4,2,3,128]{4,2,1,3,0:T(2,128)S(1)}, u32[]{:S(2)}, u32[]{:S(2)}) async-start(f32[4,4,2,3,128]{4,2,1,3,0:T(2,128)} %copy.281), calls=%async_computation.2 | async-start | bytes 98304 | tf_op jit(solution)/shard_map/all_to_all | solution.py:152
  25.5 0.1 copy.276
  25.6 0.1 reshape.2162
  25.7 0.6 gather_fusion.1
  26.3 0.0 copy-start.4
  26.3 0.1 copy.278
  26.3 0.6 copy-done.4
  26.9 0.7 %copy-done.6 = f32[24]{0:T(128)S(1)} copy-done((f32[24]{0:T(128)S(1)}, f32[24]{0:T(128)}, u32[]{:S(2)}) %copy-start.6) | copy-done | bytes 120
  27.6 0.3 fusion.91
  27.9 0.3 fusion.93
  28.3 0.0 copy-start.5
  28.3 0.3 fusion.95
  28.6 0.3 copy-done.5
  29.0 0.1 bitcast_add_fusion
  29.1 0.1 copy.274
  29.1 2.0 %all-to-all-done.2 = f32[4,4,2,3,128]{4,2,1,3,0:T(2,128)S(1)} async-done(((f32[4,4,2,3,128]{4,2,1,3,0:T(2,128)}), f32[4,4,2,3,128]{4,2,1,3,0:T(2,128)S(1)}, u32[]{:S(2)}, u32[]{:S(2)}) %all-to-all-start.2) | async-done | bytes 49184 | tf_op jit(solution)/shard_map/all_to_all | solution.py:152
  31.1 0.6 copy.282
  31.8 3.3 %all-to-all-start.3 = ((f32[4,4,2,3,128]{4,2,0,3,1:T(2,128)}), f32[4,4,2,3,128]{4,2,0,3,1:T(2,128)S(1)}, u32[]{:S(2)}, u32[]{:S(2)}) async-start(f32[4,4,2,3,128]{4,2,0,3,1:T(2,128)} %copy.282), calls=%async_computation.3 | async-start | bytes 98304 | tf_op jit(solution)/shard_map/all_to_all | solution.py:151
  35.1 0.1 copy.286
  35.2 0.7 %gather_fusion = f32[32,4,512]{2,1,0:T(4,128)S(1)} fusion(f32[64,4,512]{2,1,0:T(4,128)S(1)} %copy-done, s32[1024]{0:T(1024)S(1)} %pad_clamp_fusion.1), kind=kCustom, calls=%fused_computation | custom fusion | bytes 524416 | tf_op jit(solution)/shard_map/gather | solution.py:181
  35.9 0.2 reshape.2163
  36.1 0.1 copy.275
  36.2 2.8 %all-to-all-done.3 = f32[4,4,2,3,128]{4,2,0,3,1:T(2,128)S(1)} async-done(((f32[4,4,2,3,128]{4,2,0,3,1:T(2,128)}), f32[4,4,2,3,128]{4,2,0,3,1:T(2,128)S(1)}, u32[]{:S(2)}, u32[]{:S(2)}) %all-to-all-start.3) | async-done | bytes 49184 | tf_op jit(solution)/shard_map/all_to_all | solution.py:151
  39.1 0.3 convolution_subtract_fusion
  39.6 0.0 copy-start.2
  39.7 0.6 copy-done.2
  40.3 0.1 broadcast_multiply_fusion.5
  40.5 0.3 fusion.23
  40.9 0.3 fusion.17
  41.4 0.3 fusion.19
  41.7 0.3 fusion.21
  42.4 0.1 broadcast_multiply_fusion.2
  42.5 0.3 fusion.13
  42.9 0.3 fusion.11
  43.3 0.3 fusion.15
  43.7 0.3 fusion.9
  44.3 0.1 broadcast_add_fusion.2
  44.4 1.1 %fusion.4 = (f32[32,8,128]{2,1,0:T(8,128)S(1)}, f32[32,8,128]{2,1,0:T(8,128)S(1)}, f32[32,8,128]{2,1,0:T(8,128)S(1)}) fusion(f32[32,8,128]{2,1,0:T(8,128)S(1)} %get-tuple-element.61, f32[8,8]{1,0:T(8,128)S(1)} %add_add_fusion, pred[8,8]{1,0:T(8,128)(4,1)S(1)} %iota_compare_fusion.1, f32[32,8,128]{2,1,0:T(8,128)S(1)} %get-tuple-element.60, ...), kind=kLoop, calls=%fused_computation.14 | loop fusion | flops 2260992 | bytes 786752 | tf_op jit(solution)/shard_map/vmap()/reduce_prod | solution.py:28
  45.4 1.1 %fusion.1 = f32[32,4,128]{2,1,0:T(4,128)S(1)} fusion(f32[32,32,64]{2,1,0:T(8,128)S(1)} %reshape.2163, f32[32,8,128]{2,1,0:T(8,128)S(1)} %get-tuple-element.6, f32[32,8,128]{2,1,0:T(8,128)S(1)} %get-tuple-element.7, f32[32,8,128]{2,1,0:T(8,128)S(1)} %get-tuple-element.5), kind=kOutput, calls=%fused_computation.7 | convolution fusion | flops 101171200 | bytes 720896 | tf_op jit(solution)/shard_map/vmap()/dot_general | solution.py:114
  46.6 0.1 broadcast_select_fusion
  46.7 8.6 %all_to_all.30 = f32[4,4,2,4,128]{4,2,1,3,0:T(2,128)S(1)} all-to-all(f32[4,4,2,4,128]{4,2,1,3,0:T(2,128)S(1)} %copy.319), channel_id=1, replica_groups=mesh['groups'=2,'block'=4,'seg'=2,'sub'=2] {'block'}, dimensions={0} | all-to-all | bytes 131072 | tf_op jit(solution)/shard_map/all_to_all | solution.py:186
  55.3 0.6 %copy.320 = f32[4,4,2,4,128]{4,3,2,0,1:T(4,128)} copy(f32[4,4,2,4,128]{4,2,1,3,0:T(2,128)S(1)} %all_to_all.30) | data formatting | bytes 131072 | tf_op jit(solution)/shard_map/all_to_all | solution.py:186
  56.0 3.3 %all-to-all-start.5 = ((f32[4,4,2,4,128]{4,3,2,0,1:T(4,128)}), f32[4,4,2,4,128]{4,3,2,0,1:T(4,128)S(1)}, u32[]{:S(2)}, u32[]{:S(2)}) async-start(f32[4,4,2,4,128]{4,3,2,0,1:T(4,128)} %copy.320), calls=%async_computation.5 | async-start | bytes 131072 | tf_op jit(solution)/shard_map/all_to_all | solution.py:185
  59.3 4.1 %all-to-all-done.5 = f32[4,4,2,4,128]{4,3,2,0,1:T(4,128)S(1)} async-done(((f32[4,4,2,4,128]{4,3,2,0,1:T(4,128)}), f32[4,4,2,4,128]{4,3,2,0,1:T(4,128)S(1)}, u32[]{:S(2)}, u32[]{:S(2)}) %all-to-all-start.5) | async-done | bytes 65568 | tf_op jit(solution)/shard_map/all_to_all | solution.py:185
  63.4 1.2 %gather_fusion.2 = f32[32,4,128]{2,1,0:T(4,128)} fusion(f32[32,4,128]{2,1,0:T(4,128)S(1)} %bitcast.769, s32[1024]{0:T(1024)S(1)} %pad_clamp_fusion), kind=kCustom, calls=%fused_computation.2 | custom fusion | bytes 131200 | tf_op jit(solution)/shard_map/gather | solution.py:198
  (59 shorter events, 1.1 us)
Async XLA Ops:
  0.0 35.1 %copy-start = (f32[64,4,512]{2,1,0:T(4,128)S(1)}, f32[64,4,512]{2,1,0:T(4,128)}, u32[]{:S(2)}) copy-start(f32[64,4,512]{2,1,0:T(4,128)} %param.8) | copy-start | bytes 1572868
  1.7 7.2 %copy-start.3 = (f32[24,64]{1,0:T(8,128)S(1)}, f32[24,64]{1,0:T(8,128)}, u32[]{:S(2)}) copy-start(f32[24,64]{1,0:T(8,128)} %param.9) | copy-start | bytes 18436
  1.7 7.3 %copy-start.7 = (f32[8]{0:T(128)S(1)}, f32[8]{0:T(128)}, u32[]{:S(2)}) copy-start(f32[8]{0:T(128)} %constant.77) | copy-start | bytes 100
  1.7 7.3 %copy-start.8 = (f32[8]{0:T(128)S(1)}, f32[8]{0:T(128)}, u32[]{:S(2)}) copy-start(f32[8]{0:T(128)} %constant.75.clone) | copy-start | bytes 100
  2.4 6.7 %copy-start.1 = (f32[3,4096]{1,0:T(4,128)S(1)}, f32[3,4096]{1,0:T(4,128)}, u32[]{:S(2)}) copy-start(f32[3,4096]{1,0:T(4,128)} %param.10) | copy-start | bytes 147460
  2.4 12.1 %all-to-all-start = ((s32[4,4,2]{1,2,0:T(2,128)}), s32[4,4,2]{1,2,0:T(2,128)S(1)}, u32[]{:S(2)}, u32[]{:S(2)}) async-start(s32[4,4,2]{1,2,0:T(2,128)} %copy.272), calls=%async_computation | async-start | bytes 8192 | tf_op jit(solution)/shard_map/all_to_all | solution.py:165
  15.2 7.0 %all-to-all-start.1 = ((s32[4,4,2]{0,2,1:T(2,128)}), s32[4,4,2]{0,2,1:T(2,128)S(1)}, u32[]{:S(2)}, u32[]{:S(2)}) async-start(s32[4,4,2]{0,2,1:T(2,128)} %copy.273), calls=%async_computation.1 | async-start | bytes 8192 | tf_op jit(solution)/shard_map/all_to_all | solution.py:164
  22.2 8.9 %all-to-all-start.2 = ((f32[4,4,2,3,128]{4,2,1,3,0:T(2,128)}), f32[4,4,2,3,128]{4,2,1,3,0:T(2,128)S(1)}, u32[]{:S(2)}, u32[]{:S(2)}) async-start(f32[4,4,2,3,128]{4,2,1,3,0:T(2,128)} %copy.281), calls=%async_computation.2 | async-start | bytes 98304 | tf_op jit(solution)/shard_map/all_to_all | solution.py:152
  26.3 0.7 %copy-start.4 = (f32[2,128]{1,0:T(2,128)S(1)}, f32[2,128]{1,0:T(2,128)}, u32[]{:S(2)}) copy-start(f32[2,128]{1,0:T(2,128)} %constant.68.clone.1) | copy-start | bytes 3076
  26.9 0.7 %copy-start.6 = (f32[24]{0:T(128)S(1)}, f32[24]{0:T(128)}, u32[]{:S(2)}) copy-start(f32[24]{0:T(128)} %constant.76) | copy-start | bytes 292
  28.3 0.7 %copy-start.5 = (f32[3,8]{1,0:T(4,128)S(1)}, f32[3,8]{1,0:T(4,128)}, u32[]{:S(2)}) copy-start(f32[3,8]{1,0:T(4,128)} %constant.74.clone) | copy-start | bytes 292
  31.8 7.3 %all-to-all-start.3 = ((f32[4,4,2,3,128]{4,2,0,3,1:T(2,128)}), f32[4,4,2,3,128]{4,2,0,3,1:T(2,128)S(1)}, u32[]{:S(2)}, u32[]{:S(2)}) async-start(f32[4,4,2,3,128]{4,2,0,3,1:T(2,128)} %copy.282), calls=%async_computation.3 | async-start | bytes 98304 | tf_op jit(solution)/shard_map/all_to_all | solution.py:151
  39.6 0.7 %copy-start.2 = (f32[2,128]{1,0:T(2,128)S(1)}, f32[2,128]{1,0:T(2,128)}, u32[]{:S(2)}) copy-start(f32[2,128]{1,0:T(2,128)} %constant.73.clone.1) | copy-start | bytes 3076
  56.0 7.4 %all-to-all-start.5 = ((f32[4,4,2,4,128]{4,3,2,0,1:T(4,128)}), f32[4,4,2,4,128]{4,3,2,0,1:T(4,128)S(1)}, u32[]{:S(2)}, u32[]{:S(2)}) async-start(f32[4,4,2,4,128]{4,3,2,0,1:T(4,128)} %copy.320), calls=%async_computation.5 | async-start | bytes 131072 | tf_op jit(solution)/shard_map/all_to_all | solution.py:185
where the time goes:
time: 65.3 us; the launch traced here: 64.6 us
  starting transfers between devices  19.6 us (30%)
  waiting for transfers between devices  15.9 us (24%)
  local copies, waits for them, and re-layouts  12 us (18%)
  blocking collectives  8.63 us (13%)
  matrix products  5.16 us (8%)
  other arithmetic  2.71 us (4%)
    all_to_all x1, blocking collectives, shards(): lax.all_to_all(computed.reshape(outer_count, inner_count, CAP, var_count,...  8.63 us
    all_to_all x1, starting transfers between devices, shards(): lax.all_to_all(wanted.reshape(outer_count, inner_count, CAP), 'block', sp...  6.48 us
    all_to_all x1, waiting for transfers between devices, shards(): lax.all_to_all(lax.all_to_all(computed.reshape(outer_count, inner_count,...  4.07 us
    all_to_all x1, waiting for transfers between devices, shards(): lax.all_to_all(wanted.reshape(outer_count, inner_count, CAP), 'block', sp...  3.88 us
    all_to_all x1, starting transfers between devices, shards(): lax.all_to_all(lax.all_to_all(computed.reshape(outer_count, inner_count,...  3.28 us
    all_to_all x1, starting transfers between devices, shards(): lax.all_to_all(outgoing.reshape(outer_count, inner_count, CAP, 3, point_c...  3.27 us
    all_to_all x1, starting transfers between devices, shards(): lax.all_to_all(lax.all_to_all(outgoing.reshape(outer_count, inner_count,...  3.27 us
    all_to_all x1, starting transfers between devices, shards(): lax.all_to_all(lax.all_to_all(wanted.reshape(outer_count, inner_count, CA...  3.24 us
  transfers between devices with their start and end apart: 5, of which 5 were waited for; matrix products, arithmetic and copies ran while one was open for 8% of the time, Pallas kernels for 0%

commit v1 on v0

--- a/solution.py
+++ b/solution.py
@@ -17,6 +17,29 @@
     1.0,
 )
 EXACT = lax.Precision.HIGHEST
+
+
+def in_blocks(value, dim, size):
+    before, after = (value.shape[:dim], value.shape[dim + 1 :])
+    return jnp.moveaxis(value.reshape(*before, size, -1, *after), dim, 0)
+
+
+def in_order(pieces, dim):
+    lengths = list(pieces.shape[1:])
+    lengths[dim] *= pieces.shape[0]
+    return jnp.moveaxis(pieces, 0, dim).reshape(lengths)
+
+
+def rotated_exchange(shard, axis, split_dim, concat_dim):
+    length, here = (lax.axis_size(axis), lax.axis_index(axis))
+    blocks = in_blocks(shard, split_dim, length)
+    out = blocks
+    for hop in range(1, length):
+        target, source = ((here + hop) % length, (here - hop) % length)
+        sent = lax.dynamic_index_in_dim(blocks, target, 0)
+        other = lax.ppermute(sent, axis, [(i, (i + hop) % length) for i in range(length)])
+        out = lax.dynamic_update_slice_in_dim(out, other, source, axis=0)
+    return in_order(out, concat_dim)
 
 
 def lagrange_rows(coords):
@@ -182,7 +205,7 @@
     shifts = jnp.transpose(corner_shift[:, element])
     computed = interpolate_blocks(fields, shifts, arrived.reshape(slot_count, 3, point_count))
     computed = jnp.where(live_slot[:, None, None], computed, 0.0)
-    returned = lax.all_to_all(
+    returned = rotated_exchange(
         lax.all_to_all(
             computed.reshape(outer_count, inner_count, CAP, var_count, point_count),
             "block",
@@ -191,9 +214,8 @@
             tiled=True,
         ),
         ("seg", "sub"),
-        split_axis=1,
-        concat_axis=1,
-        tiled=True,
+        1,
+        1,
     )
     mine = returned.reshape(slot_count, var_count, point_count)[slot_index]
     return mine.transpose(1, 0, 2).reshape(var_count, -1)

time: 65.3 us -> 62.7 us (0.960)
  blocking collectives: 8.63 us -> 0 us
  waiting for transfers between devices: 15.9 us -> 19.5 us
  starting transfers between devices: 19.6 us -> 21.3 us
    all_to_all x1 -> x0, blocking collectives: 8.63 us -> none  [shards(): lax.all_to_all(computed.reshape(outer_count, inner_count, CAP, var_count,...]
    ppermute x0 -> x3, waiting for transfers between devices: none -> 2.08 us  [rotated_exchange(): lax.ppermute(sent, axis, [(i, (i + hop) % length) for i in range(length)])]
    ppermute x0 -> x3, starting transfers between devices: none -> 1.78 us  [rotated_exchange(): lax.ppermute(sent, axis, [(i, (i + hop) % length) for i in range(length)])]
    all_to_all x1, waiting for transfers between devices: 4.07 us -> 5.67 us  [shards(): lax.all_to_all(computed.reshape(outer_count, inner_count, CAP, var_count,...]
  transfers between devices with their start and end apart: 5 -> 8, of which waited for: 5 -> 7; matrix products, arithmetic and copies ran while one was open for 8% -> 9% of each run, Pallas kernels for 0% -> 0%
where the time goes in v1:
time: 62.7 us; the launch traced here: 61.5 us
  starting transfers between devices  21.3 us (34%)
  waiting for transfers between devices  19.5 us (31%)
  local copies, waits for them, and re-layouts  11.4 us (18%)
  matrix products  5.16 us (8%)
  other arithmetic  3.36 us (5%)
  between operations  0.73 us (1%)
    all_to_all x1, starting transfers between devices, shards(): lax.all_to_all(wanted.reshape(outer_count, inner_count, CAP), 'block', sp...  6.48 us
    all_to_all x1, waiting for transfers between devices, shards(): lax.all_to_all(computed.reshape(outer_count, inner_count, CAP, var_count,...  5.67 us
    all_to_all x1, waiting for transfers between devices, shards(): lax.all_to_all(wanted.reshape(outer_count, inner_count, CAP), 'block', sp...  3.88 us
    all_to_all x1, starting transfers between devices, shards(): lax.all_to_all(computed.reshape(outer_count, inner_count, CAP, var_count,...  3.28 us
    all_to_all x1, starting transfers between devices, shards(): lax.all_to_all(outgoing.reshape(outer_count, inner_count, CAP, 3, point_c...  3.27 us
    all_to_all x1, starting transfers between devices, shards(): lax.all_to_all(lax.all_to_all(outgoing.reshape(outer_count, inner_count,...  3.27 us
    all_to_all x1, starting transfers between devices, shards(): lax.all_to_all(lax.all_to_all(wanted.reshape(outer_count, inner_count, CA...  3.2 us
    all_to_all x1, waiting for transfers between devices, shards(): lax.all_to_all(lax.all_to_all(wanted.reshape(outer_count, inner_count, CA...  3.11 us
  transfers between devices with their start and end apart: 8, of which 7 were waited for; matrix products, arithmetic and copies ran while one was open for 9% of the time, Pallas kernels for 0%

profile of v1, /device:TPU:0, one launch (start us, length us, event | category | flops | bytes accessed | tf_op | source)
XLA Modules:
  0.0 61.5 jit_solution(679950996878149628)
XLA Ops:
  0.0 0.7 %multiply_subtract_fusion.2 = (s32[32]{0:T(128)S(1)}, s32[32]{0:T(128)S(1)}, s32[32]{0:T(128)S(1)}) fusion(s32[32]{0:T(128)} %param.11), kind=kLoop, calls=%fused_computation.243 | loop fusion | flops 576 | bytes 512 | tf_op jit(solution)/shard_map/sub | solution.py:153
  0.7 0.2 select_reduce_fusion
  0.9 0.7 %scatter_custom_fusion = s32[32]{0:T(128)S(1)} fusion(s32[32]{0:T(128)S(1)} %compare_select_fusion.2, s32[32]{0:T(128)S(1)} %get-tuple-element.10, s32[]{:T(128)} %constant.106.clone.1), kind=kCustom, calls=%fused_computation.245 | custom fusion | bytes 132 | tf_op jit(solution)/shard_map/scatter | solution.py:172
  1.6 0.1 reshape.2170
  1.7 0.0 copy-start.3
  1.7 0.0 copy-start.7
  1.7 0.0 copy-start.8
  1.7 0.7 %copy.171 = s32[4,4,2]{1,2,0:T(2,128)} copy(s32[4,4,2]{2,1,0:T(4,128)S(1)} %reshape.2170) | data formatting | bytes 256 | tf_op jit(solution)/shard_map/reshape | solution.py:189
  2.4 6.5 %all-to-all-start = ((s32[4,4,2]{1,2,0:T(2,128)}), s32[4,4,2]{1,2,0:T(2,128)S(1)}, u32[]{:S(2)}, u32[]{:S(2)}) async-start(s32[4,4,2]{1,2,0:T(2,128)} %copy.171), calls=%async_computation | async-start | bytes 8192 | tf_op jit(solution)/shard_map/all_to_all | solution.py:188
  8.9 0.1 copy.176
  9.0 0.1 add_add_fusion
  9.1 1.5 %scatter_fusion = f32[32,3,128]{2,1,0:T(4,128)S(1)} fusion(f32[32,3,128]{2,1,0:T(4,128)S(1)} %broadcast.575, s32[32]{0:T(128)S(1)} %compare_select_fusion.2, f32[32,3,128]{2,1,0:T(4,128)S(1)} %bitcast.802), kind=kCustom, calls=%fused_computation.4 | custom fusion | bytes 147584 | tf_op jit(solution)/shard_map/scatter | solution.py:171
  10.6 3.9 %all-to-all-done = s32[4,4,2]{1,2,0:T(2,128)S(1)} async-done(((s32[4,4,2]{1,2,0:T(2,128)}), s32[4,4,2]{1,2,0:T(2,128)S(1)}, u32[]{:S(2)}, u32[]{:S(2)}) %all-to-all-start) | async-done | bytes 160 | tf_op jit(solution)/shard_map/all_to_all | solution.py:188
  14.5 0.7 %copy.172 = s32[4,4,2]{0,2,1:T(2,128)} copy(s32[4,4,2]{1,2,0:T(2,128)S(1)} %all-to-all-done) | data formatting | bytes 256 | tf_op jit(solution)/shard_map/all_to_all | solution.py:188
  15.2 3.2 %all-to-all-start.1 = ((s32[4,4,2]{0,2,1:T(2,128)}), s32[4,4,2]{0,2,1:T(2,128)S(1)}, u32[]{:S(2)}, u32[]{:S(2)}) async-start(s32[4,4,2]{0,2,1:T(2,128)} %copy.172), calls=%async_computation.1 | async-start | bytes 8192 | tf_op jit(solution)/shard_map/all_to_all | solution.py:187
  18.4 0.6 %copy.180 = f32[4,4,2,3,128]{4,2,1,3,0:T(2,128)} copy(f32[4,4,2,3,128]{4,3,2,1,0:T(4,128)S(1)} %bitcast.780) | data formatting | bytes 98304 | tf_op jit(solution)/shard_map/reshape | solution.py:176
  19.0 3.1 %all-to-all-done.1 = s32[4,4,2]{0,2,1:T(2,128)S(1)} async-done(((s32[4,4,2]{0,2,1:T(2,128)}), s32[4,4,2]{0,2,1:T(2,128)S(1)}, u32[]{:S(2)}, u32[]{:S(2)}) %all-to-all-start.1) | async-done | bytes 160 | tf_op jit(solution)/shard_map/all_to_all | solution.py:187
  22.1 3.3 %all-to-all-start.2 = ((f32[4,4,2,3,128]{4,2,1,3,0:T(2,128)}), f32[4,4,2,3,128]{4,2,1,3,0:T(2,128)S(1)}, u32[]{:S(2)}, u32[]{:S(2)}) async-start(f32[4,4,2,3,128]{4,2,1,3,0:T(2,128)} %copy.180), calls=%async_computation.2 | async-start | bytes 98304 | tf_op jit(solution)/shard_map/all_to_all | solution.py:175
  25.4 0.1 copy.175
  25.5 0.1 reshape.2171
  25.6 0.6 gather_fusion.1
  26.2 0.1 copy.177
  26.3 0.6 copy-done.4
  26.9 0.7 %copy-done.6 = f32[24]{0:T(128)S(1)} copy-done((f32[24]{0:T(128)S(1)}, f32[24]{0:T(128)}, u32[]{:S(2)}) %copy-start.6) | copy-done | bytes 120
  27.6 0.3 fusion.91
  27.9 0.3 fusion.93
  28.3 0.0 copy-start.5
  28.3 0.3 fusion.95
  28.6 0.3 copy-done.5
  28.9 0.1 bitcast_add_fusion
  29.0 0.1 copy.173
  29.1 2.0 %all-to-all-done.2 = f32[4,4,2,3,128]{4,2,1,3,0:T(2,128)S(1)} async-done(((f32[4,4,2,3,128]{4,2,1,3,0:T(2,128)}), f32[4,4,2,3,128]{4,2,1,3,0:T(2,128)S(1)}, u32[]{:S(2)}, u32[]{:S(2)}) %all-to-all-start.2) | async-done | bytes 49184 | tf_op jit(solution)/shard_map/all_to_all | solution.py:175
  31.1 0.6 %copy.181 = f32[4,4,2,3,128]{4,2,0,3,1:T(2,128)} copy(f32[4,4,2,3,128]{4,2,1,3,0:T(2,128)S(1)} %all-to-all-done.2) | data formatting | bytes 98304 | tf_op jit(solution)/shard_map/all_to_all | solution.py:175
  31.7 3.3 %all-to-all-start.3 = ((f32[4,4,2,3,128]{4,2,0,3,1:T(2,128)}), f32[4,4,2,3,128]{4,2,0,3,1:T(2,128)S(1)}, u32[]{:S(2)}, u32[]{:S(2)}) async-start(f32[4,4,2,3,128]{4,2,0,3,1:T(2,128)} %copy.181), calls=%async_computation.3 | async-start | bytes 98304 | tf_op jit(solution)/shard_map/all_to_all | solution.py:174
  35.0 0.1 copy.185
  35.1 0.7 %gather_fusion = f32[32,4,512]{2,1,0:T(4,128)S(1)} fusion(f32[64,4,512]{2,1,0:T(4,128)S(1)} %copy-done, s32[1024]{0:T(1024)S(1)} %pad_clamp_fusion.1), kind=kCustom, calls=%fused_computation | custom fusion | bytes 524416 | tf_op jit(solution)/shard_map/gather | solution.py:204
  35.8 0.2 reshape.2172
  36.0 0.1 copy.174
  36.2 2.8 %all-to-all-done.3 = f32[4,4,2,3,128]{4,2,0,3,1:T(2,128)S(1)} async-done(((f32[4,4,2,3,128]{4,2,0,3,1:T(2,128)}), f32[4,4,2,3,128]{4,2,0,3,1:T(2,128)S(1)}, u32[]{:S(2)}, u32[]{:S(2)}) %all-to-all-start.3) | async-done | bytes 49184 | tf_op jit(solution)/shard_map/all_to_all | solution.py:174
  39.0 0.3 convolution_subtract_fusion
  39.6 0.0 copy-start.2
  39.6 0.6 %copy-done.2 = f32[2,128]{1,0:T(2,128)S(1)} copy-done((f32[2,128]{1,0:T(2,128)S(1)}, f32[2,128]{1,0:T(2,128)}, u32[]{:S(2)}) %copy-start.2) | copy-done | bytes 1048
  40.3 0.1 broadcast_multiply_fusion.5
  40.4 0.3 fusion.23
  40.9 0.3 fusion.17
  41.3 0.3 fusion.19
  41.7 0.3 fusion.21
  42.3 0.1 broadcast_multiply_fusion.2
  42.4 0.3 fusion.13
  42.8 0.3 fusion.11
  43.2 0.3 fusion.15
  43.7 0.3 fusion.9
  44.2 0.1 broadcast_add_fusion.2
  44.3 1.1 %fusion.4 = (f32[32,8,128]{2,1,0:T(8,128)S(1)}, f32[32,8,128]{2,1,0:T(8,128)S(1)}, f32[32,8,128]{2,1,0:T(8,128)S(1)}) fusion(f32[32,8,128]{2,1,0:T(8,128)S(1)} %get-tuple-element.64, f32[8,8]{1,0:T(8,128)S(1)} %add_add_fusion, pred[8,8]{1,0:T(8,128)(4,1)S(1)} %iota_compare_fusion.1, f32[32,8,128]{2,1,0:T(8,128)S(1)} %get-tuple-element.63, ...), kind=kLoop, calls=%fused_computation.14 | loop fusion | flops 2260992 | bytes 786752 | tf_op jit(solution)/shard_map/vmap()/reduce_prod | solution.py:51
  45.4 1.1 %fusion.1 = f32[32,4,128]{2,1,0:T(4,128)S(1)} fusion(f32[32,32,64]{2,1,0:T(8,128)S(1)} %reshape.2172, f32[32,8,128]{2,1,0:T(8,128)S(1)} %get-tuple-element.6, f32[32,8,128]{2,1,0:T(8,128)S(1)} %get-tuple-element.7, f32[32,8,128]{2,1,0:T(8,128)S(1)} %get-tuple-element.5), kind=kOutput, calls=%fused_computation.7 | convolution fusion | flops 101171200 | bytes 720896 | tf_op jit(solution)/shard_map/vmap()/dot_general | solution.py:137
  46.5 0.7 %broadcast_select_fusion = f32[4,4,2,4,128]{4,3,2,1,0:T(4,128)} fusion(f32[4,4,2,4,128]{4,3,2,1,0:T(4,128)S(1)} %bitcast.781, pred[4,4,2]{2,1,0:T(4,128)(4,1)S(1)} %copy.174), kind=kLoop, calls=%fused_computation.57 | loop fusion | flops 16384 | bytes 131104 | tf_op jit(solution)/shard_map/jit(_where)/select_n | solution.py:207
  47.3 3.3 %all-to-all-start.4 = ((f32[4,4,2,4,128]{4,3,2,1,0:T(4,128)}), f32[4,4,2,4,128]{4,3,2,1,0:T(4,128)S(1)}, u32[]{:S(2)}, u32[]{:S(2)}) async-start(f32[4,4,2,4,128]{4,3,2,1,0:T(4,128)} %broadcast_select_fusion), calls=%async_computation.4 | async-start | bytes 131072 | tf_op jit(solution)/shard_map/all_to_all | solution.py:209
  50.6 5.7 %all-to-all-done.4 = f32[4,4,2,4,128]{4,3,2,1,0:T(4,128)S(1)} async-done(((f32[4,4,2,4,128]{4,3,2,1,0:T(4,128)}), f32[4,4,2,4,128]{4,3,2,1,0:T(4,128)S(1)}, u32[]{:S(2)}, u32[]{:S(2)}) %all-to-all-start.4) | async-done | bytes 65568 | tf_op jit(solution)/shard_map/all_to_all | solution.py:209
  56.3 0.1 collective-permute-start
  56.4 0.1 collective-permute-start.1
  56.6 1.6 %collective-permute-start.2 = (f32[1,4,1,2,4,128]{5,4,3,0,1,2:T(4,128)S(1)}, f32[1,4,1,2,4,128]{5,4,3,0,1,2:T(4,128)S(1)}, u32[]{:S(2)}, u32[]{:S(2)}) collective-permute-start(f32[1,4,1,2,4,128]{5,4,3,0,1,2:T(4,128)S(1)} %get-tuple-element.20), channel_id=1, source_target_pairs={{0,3},{1,0},{2,1},{3,2},{4,7},{5,4},{6,5},{7,6},{8,11},{9,8},{10,9... | collective-permute-start | bytes 49160 | tf_op jit(solution)/shard_map/ppermute | solution.py:40
  58.1 1.4 %collective-permute-done = f32[1,4,1,2,4,128]{5,4,3,0,1,2:T(4,128)S(1)} collective-permute-done((f32[1,4,1,2,4,128]{5,4,3,0,1,2:T(4,128)S(1)}, f32[1,4,1,2,4,128]{5,4,3,0,1,2:T(4,128)S(1)}, u32[]{:S(2)}, u32[]{:S(2)}) %collective-permute-start) | collective-permute-done | bytes 16416 | tf_op jit(solution)/shard_map/ppermute | solution.py:40
  59.5 0.7 %collective-permute-done.1 = f32[1,4,1,2,4,128]{5,4,3,0,1,2:T(4,128)S(1)} collective-permute-done((f32[1,4,1,2,4,128]{5,4,3,0,1,2:T(4,128)S(1)}, f32[1,4,1,2,4,128]{5,4,3,0,1,2:T(4,128)S(1)}, u32[]{:S(2)}, u32[]{:S(2)}) %collective-permute-start.1) | collective-permute-done | bytes 16416 | tf_op jit(solution)/shard_map/ppermute | solution.py:40
  60.2 1.2 %gather_fusion.2 = f32[32,4,128]{2,1,0:T(4,128)} fusion(f32[32,4,128]{2,1,0:T(4,128)S(1)} %bitcast.779, s32[1024]{0:T(1024)S(1)} %pad_clamp_fusion), kind=kCustom, calls=%fused_computation.2 | custom fusion | bytes 131200 | tf_op jit(solution)/shard_map/gather | solution.py:220
  (64 shorter events, 1.1 us)
Async XLA Ops:
  0.0 35.1 %copy-start = (f32[64,4,512]{2,1,0:T(4,128)S(1)}, f32[64,4,512]{2,1,0:T(4,128)}, u32[]{:S(2)}) copy-start(f32[64,4,512]{2,1,0:T(4,128)} %param.8) | copy-start | bytes 1572868
  1.7 7.2 %copy-start.3 = (f32[24,64]{1,0:T(8,128)S(1)}, f32[24,64]{1,0:T(8,128)}, u32[]{:S(2)}) copy-start(f32[24,64]{1,0:T(8,128)} %param.9) | copy-start | bytes 18436
  1.7 7.3 %copy-start.7 = (f32[8]{0:T(128)S(1)}, f32[8]{0:T(128)}, u32[]{:S(2)}) copy-start(f32[8]{0:T(128)} %constant.131) | copy-start | bytes 100
  1.7 7.3 %copy-start.8 = (f32[8]{0:T(128)S(1)}, f32[8]{0:T(128)}, u32[]{:S(2)}) copy-start(f32[8]{0:T(128)} %constant.129.clone) | copy-start | bytes 100
  2.4 6.7 %copy-start.1 = (f32[3,4096]{1,0:T(4,128)S(1)}, f32[3,4096]{1,0:T(4,128)}, u32[]{:S(2)}) copy-start(f32[3,4096]{1,0:T(4,128)} %param.10) | copy-start | bytes 147460
  2.4 12.1 %all-to-all-start = ((s32[4,4,2]{1,2,0:T(2,128)}), s32[4,4,2]{1,2,0:T(2,128)S(1)}, u32[]{:S(2)}, u32[]{:S(2)}) async-start(s32[4,4,2]{1,2,0:T(2,128)} %copy.171), calls=%async_computation | async-start | bytes 8192 | tf_op jit(solution)/shard_map/all_to_all | solution.py:188
  15.2 7.0 %all-to-all-start.1 = ((s32[4,4,2]{0,2,1:T(2,128)}), s32[4,4,2]{0,2,1:T(2,128)S(1)}, u32[]{:S(2)}, u32[]{:S(2)}) async-start(s32[4,4,2]{0,2,1:T(2,128)} %copy.172), calls=%async_computation.1 | async-start | bytes 8192 | tf_op jit(solution)/shard_map/all_to_all | solution.py:187
  22.1 8.9 %all-to-all-start.2 = ((f32[4,4,2,3,128]{4,2,1,3,0:T(2,128)}), f32[4,4,2,3,128]{4,2,1,3,0:T(2,128)S(1)}, u32[]{:S(2)}, u32[]{:S(2)}) async-start(f32[4,4,2,3,128]{4,2,1,3,0:T(2,128)} %copy.180), calls=%async_computation.2 | async-start | bytes 98304 | tf_op jit(solution)/shard_map/all_to_all | solution.py:175
  26.2 0.7 %copy-start.4 = (f32[2,128]{1,0:T(2,128)S(1)}, f32[2,128]{1,0:T(2,128)}, u32[]{:S(2)}) copy-start(f32[2,128]{1,0:T(2,128)} %constant.117.clone.1) | copy-start | bytes 3076
  26.9 0.7 %copy-start.6 = (f32[24]{0:T(128)S(1)}, f32[24]{0:T(128)}, u32[]{:S(2)}) copy-start(f32[24]{0:T(128)} %constant.130) | copy-start | bytes 292
  28.3 0.7 %copy-start.5 = (f32[3,8]{1,0:T(4,128)S(1)}, f32[3,8]{1,0:T(4,128)}, u32[]{:S(2)}) copy-start(f32[3,8]{1,0:T(4,128)} %constant.128.clone) | copy-start | bytes 292
  31.7 7.3 %all-to-all-start.3 = ((f32[4,4,2,3,128]{4,2,0,3,1:T(2,128)}), f32[4,4,2,3,128]{4,2,0,3,1:T(2,128)S(1)}, u32[]{:S(2)}, u32[]{:S(2)}) async-start(f32[4,4,2,3,128]{4,2,0,3,1:T(2,128)} %copy.181), calls=%async_computation.3 | async-start | bytes 98304 | tf_op jit(solution)/shard_map/all_to_all | solution.py:174
  39.6 0.7 %copy-start.2 = (f32[2,128]{1,0:T(2,128)S(1)}, f32[2,128]{1,0:T(2,128)}, u32[]{:S(2)}) copy-start(f32[2,128]{1,0:T(2,128)} %constant.122.clone.1) | copy-start | bytes 3076
  47.3 9.0 %all-to-all-start.4 = ((f32[4,4,2,4,128]{4,3,2,1,0:T(4,128)}), f32[4,4,2,4,128]{4,3,2,1,0:T(4,128)S(1)}, u32[]{:S(2)}, u32[]{:S(2)}) async-start(f32[4,4,2,4,128]{4,3,2,1,0:T(4,128)} %broadcast_select_fusion), calls=%async_computation.4 | async-start | bytes 131072 | tf_op jit(solution)/shard_map/all_to_all | solution.py:209
  56.3 3.2 %collective-permute-start = (f32[1,4,1,2,4,128]{5,4,3,0,1,2:T(4,128)S(1)}, f32[1,4,1,2,4,128]{5,4,3,0,1,2:T(4,128)S(1)}, u32[]{:S(2)}, u32[]{:S(2)}) collective-permute-start(f32[1,4,1,2,4,128]{5,4,3,0,1,2:T(4,128)S(1)} %get-tuple-element.22), channel_id=1, source_target_pairs={{0,1},{1,2},{2,3},{3,0},{4,5},{5,6},{6,7},{7,4},{8,9},{9,10},{10,1... | collective-permute-start | bytes 49160 | tf_op jit(solution)/shard_map/ppermute | solution.py:40
  56.4 3.8 %collective-permute-start.1 = (f32[1,4,1,2,4,128]{5,4,3,0,1,2:T(4,128)S(1)}, f32[1,4,1,2,4,128]{5,4,3,0,1,2:T(4,128)S(1)}, u32[]{:S(2)}, u32[]{:S(2)}) collective-permute-start(f32[1,4,1,2,4,128]{5,4,3,0,1,2:T(4,128)S(1)} %get-tuple-element.21), channel_id=1, source_target_pairs={{0,2},{1,3},{2,0},{3,1},{4,6},{5,7},{6,4},{7,5},{8,10},{9,11},{10,... | collective-permute-start | bytes 49160 | tf_op jit(solution)/shard_map/ppermute | solution.py:40
  56.6 3.7 %collective-permute-start.2 = (f32[1,4,1,2,4,128]{5,4,3,0,1,2:T(4,128)S(1)}, f32[1,4,1,2,4,128]{5,4,3,0,1,2:T(4,128)S(1)}, u32[]{:S(2)}, u32[]{:S(2)}) collective-permute-start(f32[1,4,1,2,4,128]{5,4,3,0,1,2:T(4,128)S(1)} %get-tuple-element.20), channel_id=1, source_target_pairs={{0,3},{1,0},{2,1},{3,2},{4,7},{5,4},{6,5},{7,6},{8,11},{9,8},{10,9... | collective-permute-start | bytes 49160 | tf_op jit(solution)/shard_map/ppermute | solution.py:40
